TPU v7x, 32 devices: a whole 2x2x4 slice. The times are simulated.
32 devices in a mesh: dp: 8 (over z, y), mp: 2 (over core), fsdp: 2 (over x).
Axes of the slice: x: 2, y: 2, z: 4, core: 2. Of those that a mesh axis runs over, the one named last changes fastest.
Arguments:
- features: bfloat16 [5, 1024, 512], P(None, ('dp', 'fsdp')), may hold values from -6 to 6
- memory_bank: bfloat16 [512, 32, 1024], P(('dp', 'fsdp')), may hold values from -1 to 1
- memory_fill: int32 [512], P(('dp', 'fsdp')), may hold values from 0 to 32
- left_keys: bfloat16 [512, 64, 1024], P(('dp', 'fsdp'), None, 'mp'), may hold values from -400 to 400
- left_values: bfloat16 [512, 64, 1024], P(('dp', 'fsdp'), None, 'mp'), may hold values from -6 to 6
- left_length: int32 [512], P(('dp', 'fsdp')), may hold values from 0 to 64
- w_query: bfloat16 [1024, 1024], P('fsdp', 'mp'), may hold values from -0.1875 to 0.1875
- w_key: bfloat16 [1024, 1024], P('fsdp', 'mp'), may hold values from -0.1875 to 0.1875
- w_value: bfloat16 [1024, 1024], P('fsdp', 'mp'), may hold values from -0.1875 to 0.1875
- w_out: bfloat16 [1024, 1024], P('mp', 'fsdp'), may hold values from -0.1875 to 0.1875
- w_up: bfloat16 [1024, 4096], P('fsdp', 'mp'), may hold values from -0.1875 to 0.1875
- w_down: bfloat16 [4096, 1024], P('mp', 'fsdp'), may hold values from -0.09375 to 0.09375
- out_gain: float32 [1024], replicated, may hold values from 0.1 to 1.9
Outputs:
- layer_out: bfloat16 [512, 5, 1024], P(('dp', 'fsdp'))
- memory_next: bfloat16 [512, 1024], P(('dp', 'fsdp'))
- center_keys: bfloat16 [512, 4, 1024], P(('dp', 'fsdp'), None, 'mp')
- center_values: bfloat16 [512, 4, 1024], P(('dp', 'fsdp'), None, 'mp')
All inputs are finite; a program needn't handle non-finite values.
Results may differ from a plain program's by a relative error of at most 0.0095.
Values may be sent and summed in bfloat16 or wider, within the bound.
A program may use at most 128 MiB of HBM per device.

v0:
```python
import functools

import jax
import jax.numpy as jnp
from jax import lax
from jax.experimental import pallas as pl
from jax.experimental.pallas import tpu as pltpu
from jax.sharding import PartitionSpec as P

HD = 64
GROUP = 4
ROWS = 8
KEYS = 128

epsilon = 1e-05
masked_score = -1e30
MESH = pl.DeviceIdType.MESH
bf16 = jnp.bfloat16
f32 = jnp.float32


def normalize(values):
    average = jnp.mean(values, axis=-1, keepdims=True)
    centred = values - average
    variance = jnp.mean(centred * centred, axis=-1, keepdims=True)
    return centred * lax.rsqrt(variance + epsilon)


def matmul(left, right):
    return jnp.dot(left, right, preferred_element_type=f32)


def body(
    frames,
    mem_slots,
    left_slots,
    packed,
    f_ref,
    fill_ref,
    length_ref,
    gain_ref,
    mem_hbm,
    lk_hbm,
    lv_hbm,
    wq_hbm,
    wk_hbm,
    wv_hbm,
    wo_hbm,
    wu_hbm,
    wd_hbm,
    out_ref,
    mnext_ref,
    ck_ref,
    cv_ref,
    x_ref,
    outbox,
    inbox,
    far,
    own,
    mem_v,
    lk_v,
    lv_v,
    mk,
    mv,
    gk,
    gv,
    qs,
    rows_v,
    att,
    hid,
    hbuf,
    dacc,
    part,
    peer,
    send_sem,
    recv_sem,
    psend_sem,
    precv_sem,
    load_sem,
    fsend_sem,
    frecv_sem,
):
    d = lax.axis_index("dp")
    m = lax.axis_index("mp")
    f = lax.axis_index("fsdp")
    total, width = x_ref.shape
    streams = total // ROWS
    n_blocks, depth, cols = far.shape
    n_ff = (n_blocks - 4) // 2
    quarter = depth // 4
    c1 = quarter // 4
    c2 = (quarter - c1) // 2
    ybit = lax.rem(d, 2)
    zbit = lax.rem(lax.div(d, 2), 2)
    p = lax.rem(d, 4)
    py = p + 1 - 2 * ybit
    pz = p + 2 - 4 * zbit
    pd = 3 - p
    xdev = (d, m, 1 - f)
    ydev = (d + 1 - 2 * ybit, m, f)
    zdev = (d + 2 - 4 * zbit, m, f)
    mdev = (d, 1 - m, f)

    def own_hbm(b, start, size):
        r = pl.ds(pl.multiple_of(start, 16), size)
        if b < 4:
            return (wk_hbm, wv_hbm, wq_hbm, wo_hbm)[b].at[r, :]
        j = (b - 4) // 2
        if b % 2 == 0:
            return wu_hbm.at[r, pl.ds(j * cols, cols)]
        return wd_hbm.at[pl.ds(pl.multiple_of(start + j * depth, 16), size), :]

    def piece(b, start, size):
        return far.at[b, pl.ds(pl.multiple_of(start, 16), size), :]

    sends = []

    def send(src, b, start, size, dev, kind):
        copy = pltpu.make_async_remote_copy(
            src_ref=src,
            dst_ref=piece(b, start, size),
            send_sem=send_sem.at[b, kind],
            recv_sem=recv_sem.at[b, kind],
            device_id=dev,
            device_id_type=MESH,
        )
        copy.start()
        sends.append(copy)

    def arrived(b, start, size, kind):
        ref = piece(b, start, size)
        pltpu.make_async_remote_copy(
            src_ref=ref,
            dst_ref=ref,
            send_sem=send_sem.at[b, kind],
            recv_sem=recv_sem.at[b, kind],
            device_id=xdev,
            device_id_type=MESH,
        ).wait_recv()

    def load(src, dst, i):
        copy = pltpu.make_async_copy(src, dst, load_sem.at[i])
        copy.start()
        return copy

    peers = inbox.shape[0] if packed else 0
    n_fsdp = lax.axis_size("fsdp")
    me = d * n_fsdp + f

    def place(offset):
        return lax.rem(me + offset, peers)

    def device_of(index):
        return (lax.div(index, n_fsdp), m, lax.rem(index, n_fsdp))

    barrier = pltpu.get_barrier_semaphore()
    greeted = [device_of(place(o)) for o in range(1, peers)] if packed else [xdev, ydev, zdev]
    greeted.append(mdev)
    for dev in greeted:
        pl.semaphore_signal(barrier, inc=1, device_id=dev, device_id_type=MESH)

    if packed:
        pairs = outbox.shape[1]
        for k in range(pairs):
            low = f_ref[2 * k].astype(f32)
            high = f_ref[min(2 * k + 1, frames - 1)].astype(f32)
            turned = jnp.concatenate([low, high], axis=0).T.astype(bf16)
            outbox[:, k] = turned.reshape(peers, streams, turned.shape[1])

    pl.semaphore_wait(barrier, len(greeted))

    fsends = []
    for o in range(1, peers):
        copy = pltpu.make_async_remote_copy(
            src_ref=outbox.at[place(o)],
            dst_ref=inbox.at[me],
            send_sem=fsend_sem.at[o],
            recv_sem=frecv_sem.at[o],
            device_id=device_of(place(o)),
            device_id_type=MESH,
        )
        copy.start()
        fsends.append(copy)

    def send_own(b):
        if b >= n_blocks:
            return
        send(own_hbm(b, p * quarter, quarter), b, p * quarter, quarter, xdev, 0)
        send(own_hbm(b, pd * quarter, c1), b, pd * quarter, c1, xdev, 1)

    lead = 3
    for b in range(lead):
        send_own(b)

    loads = [load(own_hbm(b, 0, depth), own.at[b], b) for b in range(n_blocks)]
    mem_load = load(mem_hbm, mem_v, n_blocks)
    lk_load = load(lk_hbm, lk_v, n_blocks + 1)
    lv_load = load(lv_hbm, lv_v, n_blocks + 2)

    def pass_quarter(b):
        if b >= n_blocks:
            return
        arrived(b, p * quarter, quarter, 0)
        send_own(b + lead)
        src = piece(b, p * quarter, quarter)
        send(src, b, p * quarter, quarter, ydev, 2)
        send(src, b, p * quarter, quarter, zdev, 3)

    def pass_diagonal(b):
        if b >= n_blocks:
            return
        at_y = pz * quarter + c1
        arrived(b, pz * quarter, quarter, 3)
        send(piece(b, at_y, c2), b, at_y, c2, ydev, 4)
        at_z = py * quarter + c1 + c2
        arrived(b, py * quarter, quarter, 2)
        send(piece(b, at_z, c2), b, at_z, c2, zdev, 5)

    def complete(b):
        arrived(b, pd * quarter, c1, 1)
        arrived(b, pd * quarter + c1, c2, 4)
        arrived(b, pd * quarter + c1 + c2, c2, 5)

    def pump(b):
        pass_quarter(b)
        pass_diagonal(b - 1)

    mine = pl.ds(pl.multiple_of(f * depth, 128), depth)
    other = pl.ds(pl.multiple_of((1 - f) * depth, 128), depth)
    tile = 64

    if packed:
        inbox[pl.ds(me, 1)] = outbox[pl.ds(me, 1)]
        for o in range(1, peers):
            ref = inbox.at[lax.rem(me + peers - o, peers)]
            pltpu.make_async_remote_copy(
                src_ref=ref,
                dst_ref=ref,
                send_sem=fsend_sem.at[o],
                recv_sem=frecv_sem.at[o],
                device_id=xdev,
                device_id_type=MESH,
            ).wait_recv()
        half = inbox.shape[3] // 2
        parts = []
        for t in range(frames):
            k, side = t // 2, t % 2
            lanes = slice(side * half, side * half + half)
            parts.append(
                jnp.concatenate([inbox[i, k][:, lanes] for i in range(peers)], axis=1)
            )
        major = jnp.concatenate(parts, axis=0)
    else:
        major = f_ref[...]
    count = frames * streams
    r_id = lax.broadcasted_iota(jnp.int32, (total, count), 0)
    c_id = lax.broadcasted_iota(jnp.int32, (total, count), 1)
    frame_id = r_id % ROWS
    target = jnp.where(frame_id < frames, frame_id * streams + r_id // ROWS, -1)
    x_ref[...] = matmul(jnp.where(target == c_id, 1.0, 0.0).astype(bf16), major).astype(bf16)

    @pl.loop(0, total // tile)
    def _(i):
        r = pl.ds(pl.multiple_of(i * tile, tile), tile)
        n = normalize(x_ref[r, :].astype(f32)).astype(bf16).astype(f32)
        n3 = n.reshape(tile // ROWS, ROWS, width)
        row = lax.broadcasted_iota(jnp.int32, n3.shape, 1)
        mean = jnp.sum(jnp.where(row < GROUP, n3, 0.0), axis=1, keepdims=True) * (1.0 / GROUP)
        n3 = jnp.where(row == frames, jnp.broadcast_to(mean, n3.shape), n3)
        rows_v[r, :] = n3.reshape(tile, width).astype(bf16)

    mem_load.wait()
    pass_quarter(0)
    pump(1)

    def project(b):
        loads[b].wait()
        complete(b)
        sums = matmul(rows_v[:, mine], own[b]) + matmul(rows_v[:, other], far[b])
        return sums.astype(bf16)

    def project_memory(b, target):
        step = 256

        @pl.loop(0, mem_v.shape[0] // step)
        def _(i):
            r = pl.ds(pl.multiple_of(i * step, step), step)
            sums = matmul(mem_v[r, mine], own[b]) + matmul(mem_v[r, other], far[b])
            target[r, :] = sums.astype(bf16)

    keys = project(0)
    ck_ref[...] = keys
    gk[...] = keys.astype(f32)
    project_memory(0, mk)
    pump(2)
    vals = project(1)
    cv_ref[...] = vals
    gv[...] = vals.astype(f32)
    project_memory(1, mv)
    pump(3)
    qs[...] = project(2).astype(f32)
    lk_load.wait()
    lv_load.wait()

    heads = cols // HD
    lanes3 = lax.broadcasted_iota(jnp.int32, (heads, ROWS, cols), 2)
    head3 = lax.broadcasted_iota(jnp.int32, (heads, ROWS, cols), 0)
    head_mask = jnp.where(lanes3 // HD == head3, 1.0, 0.0).astype(f32)
    row2 = lax.broadcasted_iota(jnp.int32, (heads * ROWS, KEYS), 0)
    lane2 = lax.broadcasted_iota(jnp.int32, (heads * ROWS, KEYS), 1)
    excluded = jnp.where((row2 % ROWS == frames) & (lane2 < mem_slots), -1.0, 0.0).astype(f32)
    lane1 = lax.broadcasted_iota(jnp.int32, (1, KEYS), 1)
    left_end = mem_slots + left_slots
    pad8 = jnp.zeros((16 - ROWS, cols), f32)
    pad = jnp.zeros((KEYS - mem_slots - left_slots - 16, cols), bf16)
    scale = HD ** (-0.5)

    def gather_rows(mem_part, left_part, group_part, s):
        return jnp.concatenate(
            [
                mem_part[pl.ds(pl.multiple_of(s * mem_slots, mem_slots), mem_slots), :],
                left_part[s],
                jnp.concatenate(
                    [group_part[pl.ds(pl.multiple_of(s * ROWS, ROWS), ROWS), :], pad8], axis=0
                ).astype(bf16),
                pad,
            ],
            axis=0,
        )

    def attend(s):
        r = pl.ds(pl.multiple_of(s * ROWS, ROWS), ROWS)
        spread = (qs[r, :][None] * head_mask).reshape(heads * ROWS, cols).astype(bf16)
        k = gather_rows(mk, lk_v, gk, s)
        scores = (
            lax.dot_general(spread, k, (((1,), (1,)), ((), ())), preferred_element_type=f32) * scale
        )
        first_mem = mem_slots - fill_ref[s]
        first_left = left_end - length_ref[s]
        first = jnp.where(lane1 < mem_slots, first_mem, first_left)
        first = jnp.where(lane1 < left_end, first, 0)
        hide1 = (lane1 < first) | (lane1 >= left_end + frames)
        hide = jnp.where(hide1, -1.0, 0.0) + excluded
        scores = jnp.where(hide < 0.0, masked_score, scores)
        top = jnp.max(scores, axis=-1, keepdims=True)
        e = jnp.exp(scores - top)
        probs = (e / jnp.sum(e, axis=-1, keepdims=True)).astype(bf16)
        v = gather_rows(mv, lv_v, gv, s)
        o = matmul(probs, v).reshape(heads, ROWS, cols) * head_mask
        att[r, :] = jnp.sum(o, axis=0)

    chunks = 4
    per_chunk = streams // chunks
    unroll = 4
    for c in range(chunks):

        @pl.loop(0, per_chunk // unroll)
        def _(i):
            for u in range(unroll):
                attend(c * per_chunk + i * unroll + u)

        if c < chunks - 1:
            pump(4 + c)

    def exchange(slot):
        copy = pltpu.make_async_remote_copy(
            src_ref=part.at[slot],
            dst_ref=peer.at[slot],
            send_sem=psend_sem.at[slot],
            recv_sem=precv_sem.at[slot],
            device_id=mdev,
            device_id_type=MESH,
        )
        copy.start()
        return copy

    loads[3].wait()
    complete(3)
    attended = att[...].astype(bf16)
    part[0, :, mine] = matmul(attended, own[3]).astype(bf16)
    part[0, :, other] = matmul(attended, far[3]).astype(bf16)
    first = exchange(0)
    pump(4 + chunks - 1)
    first.wait()

    wide = 16 * ROWS

    @pl.loop(0, total // wide)
    def _(i):
        r = pl.ds(pl.multiple_of(i * wide, wide), wide)
        a = part[0, r, :].astype(f32) + peer[0, r, :].astype(f32)
        a3 = a.reshape(wide // ROWS, ROWS, width)
        row = lax.broadcasted_iota(jnp.int32, a3.shape, 1)
        memory = jnp.sum(jnp.where(row == frames, a3, 0.0), axis=1)
        s = pl.ds(pl.multiple_of(i * 16, 16), 16)
        mnext_ref[s, :] = jnp.tanh(memory).astype(bf16)
        h = x_ref[r, :].astype(f32) + a
        hid[r, :] = h
        rows_v[r, :] = normalize(h).astype(bf16)

    ahead = 4 + chunks
    for j in range(n_ff):
        b = 4 + 2 * j
        pump(ahead)
        ahead += 1
        loads[b].wait()
        complete(b)
        up = matmul(rows_v[:, mine], own[b]) + matmul(rows_v[:, other], far[b])
        hbuf[...] = jax.nn.gelu(up, approximate=True).astype(bf16)
        if ahead <= n_blocks:
            pump(ahead)
            ahead += 1
        loads[b + 1].wait()
        complete(b + 1)
        near = matmul(hbuf[...], own[b + 1])
        away = matmul(hbuf[...], far[b + 1])
        if j == 0:
            dacc[:, mine] = near
            dacc[:, other] = away
        else:
            near = dacc[:, mine] + near
            away = dacc[:, other] + away
            if j < n_ff - 1:
                dacc[:, mine] = near
                dacc[:, other] = away
            else:
                part[1, :, mine] = near.astype(bf16)
                part[1, :, other] = away.astype(bf16)

    second = exchange(1)
    second.wait()

    @pl.loop(0, total // tile)
    def _(i):
        r = pl.ds(pl.multiple_of(i * tile, tile), tile)
        y = hid[r, :] + (part[1, r, :].astype(f32) + peer[1, r, :].astype(f32))
        out_ref[r, :] = (normalize(y) * gain_ref[...]).astype(bf16)

    for copy in sends + fsends:
        copy.wait_send()


def finish(frames, rows_ref, mem_ref, keys_ref, vals_ref, out_ref, mnext_ref, ck_ref, cv_ref):
    total, width = rows_ref.shape
    streams = total // ROWS
    count = frames * streams
    r_id = lax.broadcasted_iota(jnp.int32, (count, total), 0)
    c_id = lax.broadcasted_iota(jnp.int32, (count, total), 1)
    pick = (r_id % streams) * ROWS + r_id // streams
    moved = matmul(jnp.where(pick == c_id, 1.0, 0.0).astype(bf16), rows_ref[...])
    out_ref[...] = moved.astype(bf16)
    mnext_ref[...] = mem_ref[...]
    for src, dst in ((keys_ref, ck_ref), (vals_ref, cv_ref)):
        values = src[...].astype(f32).reshape(streams, ROWS, src.shape[1])
        dst[...] = values[:, :GROUP].astype(bf16)


def shards(
    features,
    memory_bank,
    memory_fill,
    left_keys,
    left_values,
    left_length,
    w_query,
    w_key,
    w_value,
    w_out,
    w_up,
    w_down,
    out_gain,
):
    frames, width_dev, all_streams = features.shape
    streams, mem_slots, width = memory_bank.shape
    left_slots = left_keys.shape[1]
    depth, cols = w_query.shape
    n_ff = w_up.shape[1] // cols
    n_blocks = 4 + 2 * n_ff
    total = streams * ROWS
    n_dp = lax.axis_size("dp")
    n_fsdp = lax.axis_size("fsdp")
    peers = n_dp * n_fsdp
    packed = 2 * width_dev == KEYS and streams % 16 == 0
    if packed:
        feed = features
    else:
        flat = features.reshape(frames * width_dev, all_streams)
        got = lax.all_to_all(flat, ("dp", "fsdp"), split_axis=1, concat_axis=0, tiled=True)
        got = got.reshape(peers, frames, width_dev, streams)
        feed = jnp.transpose(got, (1, 3, 0, 2)).reshape(frames * streams, width)
    slots = (peers, (frames + 1) // 2, streams, KEYS) if packed else (1, 1, 16, KEYS)
    vmem = pl.BlockSpec(memory_space=pltpu.VMEM)
    hbm = pl.BlockSpec(memory_space=pl.ANY)
    smem = pl.BlockSpec(memory_space=pltpu.SMEM)
    out, mnext, ck, cv = pl.pallas_call(
        functools.partial(body, frames, mem_slots, left_slots, packed),
        out_shape=(
            jax.ShapeDtypeStruct((total, width), bf16),
            jax.ShapeDtypeStruct((streams, width), bf16),
            jax.ShapeDtypeStruct((total, cols), bf16),
            jax.ShapeDtypeStruct((total, cols), bf16),
        ),
        in_specs=[vmem, smem, smem, vmem] + [hbm] * 9,
        out_specs=(vmem,) * 4,
        scratch_shapes=[
            pltpu.VMEM((total, width), bf16),
            pltpu.VMEM(slots, bf16),
            pltpu.VMEM(slots, bf16),
            pltpu.VMEM((n_blocks, depth, cols), bf16),
            pltpu.VMEM((n_blocks, depth, cols), bf16),
            pltpu.VMEM((streams * mem_slots, width), bf16),
            pltpu.VMEM(left_keys.shape, bf16),
            pltpu.VMEM(left_keys.shape, bf16),
            pltpu.VMEM((streams * mem_slots, cols), bf16),
            pltpu.VMEM((streams * mem_slots, cols), bf16),
            pltpu.VMEM((total, cols), f32),
            pltpu.VMEM((total, cols), f32),
            pltpu.VMEM((total, cols), f32),
            pltpu.VMEM((total, width), bf16),
            pltpu.VMEM((total, cols), f32),
            pltpu.VMEM((total, width), f32),
            pltpu.VMEM((total, cols), bf16),
            pltpu.VMEM((total, width), f32),
            pltpu.VMEM((2, total, width), bf16),
            pltpu.VMEM((2, total, width), bf16),
            pltpu.SemaphoreType.DMA((n_blocks, 6)),
            pltpu.SemaphoreType.DMA((n_blocks, 6)),
            pltpu.SemaphoreType.DMA((2,)),
            pltpu.SemaphoreType.DMA((2,)),
            pltpu.SemaphoreType.DMA((n_blocks + 3,)),
            pltpu.SemaphoreType.DMA((peers,)),
            pltpu.SemaphoreType.DMA((peers,)),
        ],
        compiler_params=pltpu.CompilerParams(
            collective_id=0, has_side_effects=True, vmem_limit_bytes=60 * 1024 * 1024
        ),
    )(
        feed,
        memory_fill,
        left_length,
        out_gain.reshape(1, width),
        memory_bank.reshape(streams * mem_slots, width),
        left_keys,
        left_values,
        w_query,
        w_key,
        w_value,
        w_out,
        w_up,
        w_down,
    )
    layer_out, memory_next, center_keys, center_values = pl.pallas_call(
        functools.partial(finish, frames),
        out_shape=(
            jax.ShapeDtypeStruct((frames * streams, width), bf16),
            jax.ShapeDtypeStruct((streams, width), bf16),
            jax.ShapeDtypeStruct((streams, GROUP, cols), bf16),
            jax.ShapeDtypeStruct((streams, GROUP, cols), bf16),
        ),
        in_specs=[vmem] * 4,
        out_specs=(vmem,) * 4,
    )(out, mnext, ck, cv)
    layer_out = jnp.transpose(layer_out.reshape(frames, streams, width), (1, 0, 2))
    return (layer_out, memory_next, center_keys, center_values)


def solution(mesh):
    in_specs = (
        P(None, ("dp", "fsdp"), None),
        P(("dp", "fsdp"), None, None),
        P(("dp", "fsdp")),
        P(("dp", "fsdp"), None, "mp"),
        P(("dp", "fsdp"), None, "mp"),
        P(("dp", "fsdp")),
        P("fsdp", "mp"),
        P("fsdp", "mp"),
        P("fsdp", "mp"),
        P("mp", "fsdp"),
        P("fsdp", "mp"),
        P("mp", "fsdp"),
        P(),
    )
    out_specs = (
        P(("dp", "fsdp"), None, None),
        P(("dp", "fsdp"), None),
        P(("dp", "fsdp"), None, "mp"),
        P(("dp", "fsdp"), None, "mp"),
    )
    return jax.shard_map(shards, mesh=mesh, in_specs=in_specs, out_specs=out_specs, check_vma=False)
```

profile of v0, /device:TPU:0, one launch (start us, length us, event | category | flops | bytes accessed | tf_op | source)
XLA Modules:
  0.0 87.2 jit_solution(4153380937306748438)
XLA Ops:
  0.6 84.4 %shard_map.156 = (bf16[256,1024]{1,0:T(8,128)(2,1)}, bf16[32,1024]{1,0:T(8,128)(2,1)}, bf16[256,512]{1,0:T(8,128)(2,1)}, bf16[256,512]{1,0:T(8,128)(2,1)}) custom-call(bf16[5,64,512]{2,1,0:T(8,128)(2,1)} %f_ref.1, s32[32]{0:T(128)} %fill_ref.1, s32[32]{0:T(128)} %length_ref.1, f32[1,1024]{1,0:T(1,128)} %bitcast.6, bf16[1024,1024]{1,0:T(8,128)(2,1)} %bitcast.5, ...), custom_call_target="tpu_custom_call" | custom-call | tf_op jit(solution)/shard_map/pallas_call | solution.py:495
  85.0 2.2 %shard_map.157 = (bf16[160,1024]{1,0:T(8,128)(2,1)}, bf16[32,1024]{1,0:T(8,128)(2,1)}, bf16[32,4,512]{2,1,0:T(4,128)(2,1)}, bf16[32,4,512]{2,1,0:T(4,128)(2,1)}) custom-call(bf16[256,1024]{1,0:T(8,128)(2,1)} %get-tuple-element.12.rows_ref, bf16[32,1024]{1,0:T(8,128)(2,1)} %get-tuple-element.13.mem_ref, bf16[256,512]{1,0:T(8,128)(2,1)} %get-tuple-element.14.keys_ref, ...), custom_call_target="tpu_custom_call" | custom-call | tf_op jit(solution)/shard_map/pallas_call | solution.py:552
where the time goes:
time: 87.4 us; the launch traced here: 87.2 us
  Pallas kernels  86.6 us (99%)
    pallas_call x1, Pallas kernels, shards(): pl.pallas_call(functools.partial(body, frames, mem_slots, left_slots, pac...  84.4 us
    pallas_call x1, Pallas kernels, shards(): pl.pallas_call(functools.partial(finish, frames), out_shape=(jax.ShapeDty...  2.24 us

commit v1 on v0

v1 whole, which is shorter than its diff:
```python
import functools

import jax
import jax.numpy as jnp
from jax import lax
from jax.experimental import pallas as pl
from jax.experimental.pallas import tpu as pltpu
from jax.sharding import PartitionSpec as P

HD = 64
GROUP = 4
ROWS = 8
KEYS = 128
LEAD = 3

epsilon = 1e-05
masked_score = -1e30
MESH = pl.DeviceIdType.MESH
bf16 = jnp.bfloat16
f32 = jnp.float32


def normalize(values):
    average = jnp.mean(values, axis=-1, keepdims=True)
    centred = values - average
    variance = jnp.mean(centred * centred, axis=-1, keepdims=True)
    return centred * lax.rsqrt(variance + epsilon)


def matmul(left, right):
    return jnp.dot(left, right, preferred_element_type=f32)


def body(
    frames,
    mem_slots,
    left_slots,
    packed,
    f_hbm,
    fill_hbm,
    length_hbm,
    gain_hbm,
    mem_hbm,
    lk_hbm,
    lv_hbm,
    wq_hbm,
    wk_hbm,
    wv_hbm,
    wo_hbm,
    wu_hbm,
    wd_hbm,
    out_ref,
    mnext_ref,
    ck_ref,
    cv_ref,
    f_ref,
    fill_ref,
    length_ref,
    gain_ref,
    x_ref,
    outbox,
    inbox,
    far,
    own,
    mem_v,
    lk_v,
    lv_v,
    mk,
    mv,
    gk,
    gv,
    qs,
    rows_v,
    att,
    hid,
    hn,
    hn_far,
    act,
    act_far,
    dacc,
    dacc_far,
    part,
    peer,
    stage_out,
    stage_in,
    send_sem,
    recv_sem,
    psend_sem,
    precv_sem,
    load_sem,
    fsend_sem,
    frecv_sem,
    gsend_sem,
    grecv_sem,
    hello,
):
    d = lax.axis_index("dp")
    m = lax.axis_index("mp")
    f = lax.axis_index("fsdp")
    total, width = rows_v.shape
    streams = total // ROWS
    count = frames * streams
    half = count // 2
    n_blocks, depth, cols = far.shape
    n_ff = (n_blocks - 4) // 2
    n_hid = n_ff * cols
    quarter = depth // 4
    c1 = quarter // 4
    c2 = (quarter - c1) // 2
    ybit = lax.rem(d, 2)
    zbit = lax.rem(lax.div(d, 2), 2)
    p = lax.rem(d, 4)
    py = p + 1 - 2 * ybit
    pz = p + 2 - 4 * zbit
    pd = 3 - p
    xdev = (d, m, 1 - f)
    ydev = (d + 1 - 2 * ybit, m, f)
    zdev = (d + 2 - 4 * zbit, m, f)
    mdev = (d, 1 - m, f)

    def own_hbm(b, start, size, side):
        r = pl.ds(pl.multiple_of(start, 16), size)
        if b < 4:
            return (wk_hbm, wv_hbm, wq_hbm, wo_hbm)[b].at[r, :]
        j = (b - 4) // 2
        first = side * n_hid + j * cols
        if b % 2 == 0:
            return wu_hbm.at[r, pl.ds(pl.multiple_of(first, 128), cols)]
        return wd_hbm.at[pl.ds(pl.multiple_of(start + first, 16), size), :]

    def piece(b, start, size):
        return far.at[b, pl.ds(pl.multiple_of(start, 16), size), :]

    sends = []

    def push(src, dst, s_sem, r_sem, dev):
        copy = pltpu.make_async_remote_copy(
            src_ref=src,
            dst_ref=dst,
            send_sem=s_sem,
            recv_sem=r_sem,
            device_id=dev,
            device_id_type=MESH,
        )
        copy.start()
        sends.append(copy)
        return copy

    def landed(ref, s_sem, r_sem):
        pltpu.make_async_remote_copy(
            src_ref=ref,
            dst_ref=ref,
            send_sem=s_sem,
            recv_sem=r_sem,
            device_id=xdev,
            device_id_type=MESH,
        ).wait_recv()

    def send(src, b, start, size, dev, kind):
        push(src, piece(b, start, size), send_sem.at[b, kind], recv_sem.at[b, kind], dev)

    def arrived(b, start, size, kind):
        landed(piece(b, start, size), send_sem.at[b, kind], recv_sem.at[b, kind])

    def load(src, dst, i):
        copy = pltpu.make_async_copy(src, dst, load_sem.at[i])
        copy.start()
        return copy

    peers = inbox.shape[0] if packed else 0
    n_fsdp = lax.axis_size("fsdp")
    me = d * n_fsdp + f

    def place(offset):
        return lax.rem(me + offset, peers)

    def device_of(index):
        return (lax.div(index, n_fsdp), m, lax.rem(index, n_fsdp))

    barrier = pltpu.get_barrier_semaphore()
    greeted = [xdev, ydev, zdev, mdev]
    if packed:
        wbit = lax.rem(lax.div(d, 4), 2)
        greeted.append((d + 4 - 8 * wbit, m, f))
    for dev in greeted:
        pl.semaphore_signal(barrier, inc=1, device_id=dev, device_id_type=MESH)

    f_load = load(f_hbm, f_ref if packed else x_ref, n_blocks + 3)
    small_loads = [
        load(fill_hbm, fill_ref, n_blocks + 4),
        load(length_hbm, length_ref, n_blocks + 5),
        load(gain_hbm, gain_ref, n_blocks + 6),
    ]

    if packed:
        f_load.wait()
        pairs = outbox.shape[1]
        for k in range(pairs):
            low = f_ref[2 * k].astype(f32)
            high = f_ref[min(2 * k + 1, frames - 1)].astype(f32)
            turned = jnp.concatenate([low, high], axis=0).T.astype(bf16)
            outbox[:, k] = turned.reshape(peers, streams, turned.shape[1])

    with jax.named_scope("barwait"):
        pl.semaphore_wait(barrier, len(greeted))

    def send_quarter(b):
        send(own_hbm(b, p * quarter, quarter, 1 - f), b, p * quarter, quarter, xdev, 0)

    def send_rest(b):
        send(own_hbm(b, pd * quarter, c1, 1 - f), b, pd * quarter, c1, xdev, 1)

    def send_own(b):
        if b >= n_blocks:
            return
        send_quarter(b)
        send_rest(b)

    send_quarter(0)
    share = streams // 2

    def slot(box, i, side):
        return box.at[i, :, pl.ds(pl.multiple_of(side * share, 16), share), :]

    if packed:
        for i, dev in enumerate((zdev, ydev, xdev)):
            with jax.named_scope("hello%d" % i):
                pl.semaphore_signal(hello.at[i], inc=1, device_id=dev, device_id_type=MESH)
                pl.semaphore_wait(hello.at[i], 1)
        for o in range(1, peers):
            push(
                slot(outbox, place(o), m),
                slot(inbox, me, m),
                fsend_sem.at[o],
                frecv_sem.at[o],
                device_of(place(o)),
            )
    send_rest(0)
    for b in range(1, LEAD):
        send_own(b)

    loads = [load(own_hbm(b, 0, depth, f), own.at[b], b) for b in range(n_blocks)]
    mem_load = load(mem_hbm, mem_v, n_blocks)
    lk_load = load(lk_hbm, lk_v, n_blocks + 1)
    lv_load = load(lv_hbm, lv_v, n_blocks + 2)

    def pass_quarter(b):
        if b >= n_blocks:
            return
        arrived(b, p * quarter, quarter, 0)
        send_own(b + LEAD)
        src = piece(b, p * quarter, quarter)
        send(src, b, p * quarter, quarter, ydev, 2)
        send(src, b, p * quarter, quarter, zdev, 3)

    def pass_diagonal(b):
        if b >= n_blocks:
            return
        at_y = pz * quarter + c1
        arrived(b, pz * quarter, quarter, 3)
        send(piece(b, at_y, c2), b, at_y, c2, ydev, 4)
        at_z = py * quarter + c1 + c2
        arrived(b, py * quarter, quarter, 2)
        send(piece(b, at_z, c2), b, at_z, c2, zdev, 5)

    def complete(b):
        loads[b].wait()
        arrived(b, pd * quarter, c1, 1)
        arrived(b, pd * quarter + c1, c2, 4)
        arrived(b, pd * quarter + c1 + c2, c2, 5)

    def pump(b):
        pass_diagonal(b - 2)
        pass_quarter(b)

    mine = pl.ds(pl.multiple_of(f * depth, 128), depth)
    other = pl.ds(pl.multiple_of((1 - f) * depth, 128), depth)

    with jax.named_scope("r01"):
        pass_quarter(0)
        pass_quarter(1)

    if packed:
        inbox[pl.ds(me, 1)] = outbox[pl.ds(me, 1)]
        with jax.named_scope("fwait"):
            for o in range(1, peers):
                ref = slot(inbox, lax.rem(me + peers - o, peers), m)
                landed(ref, fsend_sem.at[o], frecv_sem.at[o])
                push(ref, ref, gsend_sem.at[o], grecv_sem.at[o], mdev)
        with jax.named_scope("gwait"):
            for o in range(1, peers):
                ref = slot(inbox, lax.rem(me + peers - o, peers), 1 - m)
                landed(ref, gsend_sem.at[o], grecv_sem.at[o])
        lane_half = inbox.shape[3] // 2
        for t in range(frames):
            k, side = t // 2, t % 2
            lanes = slice(side * lane_half, side * lane_half + lane_half)
            x_ref[t * streams : (t + 1) * streams, :] = jnp.concatenate(
                [inbox[i, k][:, lanes] for i in range(peers)], axis=1
            )
    else:
        f_load.wait()

    with jax.named_scope("norm"):
        summed = None
        major = []
        for t in range(frames):
            n = normalize(x_ref[t * streams : (t + 1) * streams, :].astype(f32)).astype(bf16)
            major.append(n)
            if t < GROUP:
                summed = n.astype(f32) if t == 0 else summed + n.astype(f32)
        major.append((summed * (1.0 / GROUP)).astype(bf16))
        major = jnp.concatenate(major, axis=0)
        packed_rows = count + streams
        r_id = lax.broadcasted_iota(jnp.int32, (total, packed_rows), 0)
        c_id = lax.broadcasted_iota(jnp.int32, (total, packed_rows), 1)
        frame_id = r_id % ROWS
        target = jnp.where(frame_id <= frames, frame_id * streams + r_id // ROWS, -1)
        spread_rows = jnp.where(target == c_id, 1.0, 0.0).astype(bf16)
        rows_v[...] = matmul(spread_rows, major).astype(bf16)

    with jax.named_scope("pump2"):
        pump(2)
        mem_load.wait()

    def project(b):
        with jax.named_scope("c%d" % b):
            complete(b)
        sums = matmul(rows_v[:, mine], own[b]) + matmul(rows_v[:, other], far[b])
        return sums.astype(bf16)

    def project_memory(b, target):
        step = 256

        @pl.loop(0, mem_v.shape[0] // step)
        def _(i):
            r = pl.ds(pl.multiple_of(i * step, step), step)
            sums = matmul(mem_v[r, mine], own[b]) + matmul(mem_v[r, other], far[b])
            target[r, :] = sums.astype(bf16)

    keys = project(0).astype(f32)
    gk[...] = keys
    ck_ref[...] = keys.reshape(streams, ROWS, cols)[:, :GROUP].astype(bf16)
    project_memory(0, mk)
    with jax.named_scope("pump3"):
        pump(3)
    vals = project(1).astype(f32)
    gv[...] = vals
    cv_ref[...] = vals.reshape(streams, ROWS, cols)[:, :GROUP].astype(bf16)
    project_memory(1, mv)
    with jax.named_scope("pump4"):
        pump(4)
    qs[...] = project(2).astype(f32)
    for copy in [lk_load, lv_load] + small_loads:
        copy.wait()

    heads = cols // HD
    lanes3 = lax.broadcasted_iota(jnp.int32, (heads, ROWS, cols), 2)
    head3 = lax.broadcasted_iota(jnp.int32, (heads, ROWS, cols), 0)
    head_mask = jnp.where(lanes3 // HD == head3, 1.0, 0.0).astype(f32)
    row2 = lax.broadcasted_iota(jnp.int32, (heads * ROWS, KEYS), 0)
    lane2 = lax.broadcasted_iota(jnp.int32, (heads * ROWS, KEYS), 1)
    excluded = jnp.where((row2 % ROWS == frames) & (lane2 < mem_slots), -1.0, 0.0).astype(f32)
    lane1 = lax.broadcasted_iota(jnp.int32, (1, KEYS), 1)
    left_end = mem_slots + left_slots
    pad8 = jnp.zeros((16 - ROWS, cols), f32)
    pad = jnp.zeros((KEYS - mem_slots - left_slots - 16, cols), bf16)
    scale = HD ** (-0.5)

    def gather_rows(mem_part, left_part, group_part, s):
        return jnp.concatenate(
            [
                mem_part[pl.ds(pl.multiple_of(s * mem_slots, mem_slots), mem_slots), :],
                left_part[s],
                jnp.concatenate(
                    [group_part[pl.ds(pl.multiple_of(s * ROWS, ROWS), ROWS), :], pad8], axis=0
                ).astype(bf16),
                pad,
            ],
            axis=0,
        )

    def attend(s):
        r = pl.ds(pl.multiple_of(s * ROWS, ROWS), ROWS)
        spread = (qs[r, :][None] * head_mask).reshape(heads * ROWS, cols).astype(bf16)
        k = gather_rows(mk, lk_v, gk, s)
        scores = (
            lax.dot_general(spread, k, (((1,), (1,)), ((), ())), preferred_element_type=f32) * scale
        )
        first_mem = mem_slots - fill_ref[s]
        first_left = left_end - length_ref[s]
        first = jnp.where(lane1 < mem_slots, first_mem, first_left)
        first = jnp.where(lane1 < left_end, first, 0)
        hide1 = (lane1 < first) | (lane1 >= left_end + frames)
        hide = jnp.where(hide1, -1.0, 0.0) + excluded
        scores = jnp.where(hide < 0.0, masked_score, scores)
        top = jnp.max(scores, axis=-1, keepdims=True)
        e = jnp.exp(scores - top)
        probs = (e / jnp.sum(e, axis=-1, keepdims=True)).astype(bf16)
        v = gather_rows(mv, lv_v, gv, s)
        o = matmul(probs, v).reshape(heads, ROWS, cols) * head_mask
        att[r, :] = jnp.sum(o, axis=0)

    chunks = 4
    per_chunk = streams // chunks
    unroll = 4
    for c in range(chunks):
        with jax.named_scope("att%d" % c):

            @pl.loop(0, per_chunk // unroll)
            def _(i):
                for u in range(unroll):
                    attend(c * per_chunk + i * unroll + u)

        with jax.named_scope("apump%d" % c):
            if c != 2:
                pump(5 + min(c, 2))

    with jax.named_scope("c3"):
        complete(3)
    with jax.named_scope("oproj"):
        r_id = lax.broadcasted_iota(jnp.int32, (packed_rows, total), 0)
        c_id = lax.broadcasted_iota(jnp.int32, (packed_rows, total), 1)
        pick = (r_id % streams) * ROWS + r_id // streams
        gather = jnp.where(pick == c_id, 1.0, 0.0).astype(bf16)
        attended = matmul(gather, att[...].astype(bf16)).astype(bf16)
        part[:, mine] = matmul(attended, own[3]).astype(bf16)
        part[:, other] = matmul(attended, far[3]).astype(bf16)
    push(part, peer, psend_sem.at[0], precv_sem.at[0], mdev)
    with jax.named_scope("d6"):
        for b in range(6, n_blocks - 1):
            pass_diagonal(b)
            pass_quarter(b + 2)
    with jax.named_scope("ex0"):
        landed(peer, psend_sem.at[0], precv_sem.at[0])

    my_half = pl.multiple_of(m * half, 16)
    its_half = pl.multiple_of((1 - m) * half, 16)

    def residual(start):
        r = pl.ds(start, half)
        h = x_ref[r, :].astype(f32) + (part[r, :].astype(f32) + peer[r, :].astype(f32))
        hid[r, :] = h
        hn[r, :] = normalize(h).astype(bf16)

    with jax.named_scope("hid"):
        residual(my_half)
        rows_mine = pl.ds(my_half, half)
        rows_its = pl.ds(its_half, half)
        push(
            hn.at[rows_mine, :], hn_far.at[rows_mine, :], psend_sem.at[1], precv_sem.at[1], xdev
        )
        residual(its_half)
        s = slice(count, packed_rows)
        mnext_ref[...] = jnp.tanh(part[s, :].astype(f32) + peer[s, :].astype(f32)).astype(bf16)

    def up(rows, target, j):
        sums = matmul(rows[:, mine], own[4 + 2 * j]) + matmul(rows[:, other], far[4 + 2 * j])
        target[:, j * cols : (j + 1) * cols] = jax.nn.gelu(sums, approximate=True).astype(bf16)

    def down(rows, target, j):
        hidden = rows[:, j * cols : (j + 1) * cols]
        for sel, weights in ((mine, own), (other, far)):
            sums = matmul(hidden, weights[5 + 2 * j])
            target[:, sel] = sums if j == 0 else target[:, sel] + sums

    for j in range(n_ff):
        with jax.named_scope("c_up%d" % j):
            complete(4 + 2 * j)
        with jax.named_scope("up%d" % j):
            up(hn, act, j)
        if j < n_ff - 1:
            with jax.named_scope("c_dn%d" % j):
                complete(5 + 2 * j)
            with jax.named_scope("dn%d" % j):
                down(act, dacc, j)
        if j == 0:
            with jax.named_scope("d7"):
                pass_diagonal(n_blocks - 1)
    with jax.named_scope("hnwait"):
        landed(hn_far.at[rows_mine, :], psend_sem.at[1], precv_sem.at[1])
        push(
            hn_far.at[rows_mine, :],
            hn_far.at[rows_mine, :],
            psend_sem.at[2],
            precv_sem.at[2],
            mdev,
        )
        landed(hn_far.at[rows_its, :], psend_sem.at[2], precv_sem.at[2])
    with jax.named_scope("farup"):
        for j in range(n_ff):
            up(hn_far, act_far, j)
    with jax.named_scope("c7"):
        complete(n_blocks - 1)
    with jax.named_scope("fardn"):
        for j in range(n_ff):
            down(act_far, dacc_far, j)
        stage_out[0] = dacc_far[rows_its, :].astype(bf16)
    push(stage_out.at[0], stage_in.at[0], psend_sem.at[3], precv_sem.at[3], mdev)
    with jax.named_scope("dnlast"):
        down(act, dacc, n_ff - 1)
        stage_out[1] = dacc[rows_its, :].astype(bf16)
    push(stage_out.at[1], stage_in.at[1], psend_sem.at[4], precv_sem.at[4], mdev)
    with jax.named_scope("xsum"):
        landed(stage_in.at[0], psend_sem.at[3], precv_sem.at[3])
        stage_out[2] = (dacc_far[rows_mine, :] + stage_in[0].astype(f32)).astype(bf16)
    push(stage_out.at[2], stage_in.at[2], psend_sem.at[5], precv_sem.at[5], xdev)
    with jax.named_scope("ownsum"):
        landed(stage_in.at[1], psend_sem.at[4], precv_sem.at[4])
        hid[rows_mine, :] = hid[rows_mine, :] + (dacc[rows_mine, :] + stage_in[1].astype(f32))
    with jax.named_scope("xwait"):
        landed(stage_in.at[2], psend_sem.at[5], precv_sem.at[5])
    with jax.named_scope("final"):
        y = hid[rows_mine, :] + stage_in[2].astype(f32)
        y = (normalize(y) * gain_ref[...]).astype(bf16)
        stage_out[3] = y
        out_ref[rows_mine, :] = y
    push(stage_out.at[3], stage_in.at[3], psend_sem.at[6], precv_sem.at[6], mdev)
    with jax.named_scope("lastwait"):
        landed(stage_in.at[3], psend_sem.at[6], precv_sem.at[6])
        out_ref[rows_its, :] = stage_in[3]

    with jax.named_scope("sendwait"):
        for copy in sends:
            copy.wait_send()


def finish(rows_ref, mem_ref, keys_ref, vals_ref, out_ref, mnext_ref, ck_ref, cv_ref):
    out_ref[...] = rows_ref[...]
    mnext_ref[...] = mem_ref[...]
    ck_ref[...] = keys_ref[...]
    cv_ref[...] = vals_ref[...]


def shards(
    features,
    memory_bank,
    memory_fill,
    left_keys,
    left_values,
    left_length,
    w_query,
    w_key,
    w_value,
    w_out,
    w_up,
    w_down,
    out_gain,
):
    frames, width_dev, all_streams = features.shape
    streams, mem_slots, width = memory_bank.shape
    left_slots = left_keys.shape[1]
    depth, cols = w_query.shape
    n_dp = lax.axis_size("dp")
    n_fsdp = lax.axis_size("fsdp")
    n_ff = w_up.shape[1] // (n_fsdp * cols)
    n_blocks = 4 + 2 * n_ff
    total = streams * ROWS
    count = frames * streams
    peers = n_dp * n_fsdp
    packed = 2 * width_dev == KEYS and streams % 32 == 0 and n_dp == 8 and n_fsdp == 2
    if packed:
        feed = features
    else:
        flat = features.reshape(frames * width_dev, all_streams)
        got = lax.all_to_all(flat, ("dp", "fsdp"), split_axis=1, concat_axis=0, tiled=True)
        got = got.reshape(peers, frames, width_dev, streams)
        feed = jnp.transpose(got, (1, 3, 0, 2)).reshape(count, width)
    slots = (peers, (frames + 1) // 2, streams, KEYS) if packed else (1, 1, 32, KEYS)
    vmem = pl.BlockSpec(memory_space=pltpu.VMEM)
    hbm = pl.BlockSpec(memory_space=pl.ANY)
    results = (
        ((count, width), bf16),
        ((streams, width), bf16),
        ((streams, GROUP, cols), bf16),
        ((streams, GROUP, cols), bf16),
    )
    middle = pl.pallas_call(
        functools.partial(body, frames, mem_slots, left_slots, packed),
        out_shape=tuple(jax.ShapeDtypeStruct(*r) for r in results),
        in_specs=[hbm] * 13,
        out_specs=(vmem,) * 4,
        scratch_shapes=[
            pltpu.VMEM(features.shape if packed else (1, 16, KEYS), bf16),
            pltpu.SMEM((streams,), jnp.int32),
            pltpu.SMEM((streams,), jnp.int32),
            pltpu.VMEM((1, width), f32),
            pltpu.VMEM((count, width), bf16),
            pltpu.VMEM(slots, bf16),
            pltpu.VMEM(slots, bf16),
            pltpu.VMEM((n_blocks, depth, cols), bf16),
            pltpu.VMEM((n_blocks, depth, cols), bf16),
            pltpu.VMEM((streams * mem_slots, width), bf16),
            pltpu.VMEM(left_keys.shape, bf16),
            pltpu.VMEM(left_keys.shape, bf16),
            pltpu.VMEM((streams * mem_slots, cols), bf16),
            pltpu.VMEM((streams * mem_slots, cols), bf16),
            pltpu.VMEM((total, cols), f32),
            pltpu.VMEM((total, cols), f32),
            pltpu.VMEM((total, cols), f32),
            pltpu.VMEM((total, width), bf16),
            pltpu.VMEM((total, cols), f32),
            pltpu.VMEM((count, width), f32),
            pltpu.VMEM((count, width), bf16),
            pltpu.VMEM((count, width), bf16),
            pltpu.VMEM((count, n_ff * cols), bf16),
            pltpu.VMEM((count, n_ff * cols), bf16),
            pltpu.VMEM((count, width), f32),
            pltpu.VMEM((count, width), f32),
            pltpu.VMEM((count + streams, width), bf16),
            pltpu.VMEM((count + streams, width), bf16),
            pltpu.VMEM((4, count // 2, width), bf16),
            pltpu.VMEM((4, count // 2, width), bf16),
            pltpu.SemaphoreType.DMA((n_blocks, 6)),
            pltpu.SemaphoreType.DMA((n_blocks, 6)),
            pltpu.SemaphoreType.DMA((7,)),
            pltpu.SemaphoreType.DMA((7,)),
            pltpu.SemaphoreType.DMA((n_blocks + 7,)),
            pltpu.SemaphoreType.DMA((peers,)),
            pltpu.SemaphoreType.DMA((peers,)),
            pltpu.SemaphoreType.DMA((peers,)),
            pltpu.SemaphoreType.DMA((peers,)),
            pltpu.SemaphoreType.REGULAR((3,)),
        ],
        compiler_params=pltpu.CompilerParams(
            collective_id=0, has_side_effects=True, vmem_limit_bytes=60 * 1024 * 1024
        ),
    )(
        feed,
        memory_fill,
        left_length,
        out_gain.reshape(1, width),
        memory_bank.reshape(streams * mem_slots, width),
        left_keys,
        left_values,
        w_query,
        w_key,
        w_value,
        w_out,
        w_up,
        w_down,
    )
    layer_out, memory_next, center_keys, center_values = pl.pallas_call(
        finish,
        out_shape=tuple(jax.ShapeDtypeStruct(*r) for r in results),
        in_specs=[vmem] * 4,
        out_specs=(vmem,) * 4,
    )(*middle)
    layer_out = jnp.transpose(layer_out.reshape(frames, streams, width), (1, 0, 2))
    return (layer_out, memory_next, center_keys, center_values)


def solution(mesh):
    in_specs = (
        P(None, ("dp", "fsdp"), None),
        P(("dp", "fsdp"), None, None),
        P(("dp", "fsdp")),
        P(("dp", "fsdp"), None, "mp"),
        P(("dp", "fsdp"), None, "mp"),
        P(("dp", "fsdp")),
        P("fsdp", "mp"),
        P("fsdp", "mp"),
        P("fsdp", "mp"),
        P("mp", "fsdp"),
        P("fsdp", "mp"),
        P("mp", "fsdp"),
        P(),
    )
    out_specs = (
        P(("dp", "fsdp"), None, None),
        P(("dp", "fsdp"), None),
        P(("dp", "fsdp"), None, "mp"),
        P(("dp", "fsdp"), None, "mp"),
    )
    return jax.shard_map(shards, mesh=mesh, in_specs=in_specs, out_specs=out_specs, check_vma=False)
```

time: 87.4 us -> 67.1 us (0.77)
  Pallas kernels: 86.6 us -> 66.2 us
    pallas_call x1, Pallas kernels: 84.4 us -> 64.3 us  [shards(): pl.pallas_call(functools.partial(body, frames, mem_slots, left_slots, pac...]
where the time goes in v1:
time: 67.1 us; the launch traced here: 66.9 us
  Pallas kernels  66.2 us (99%)
    pallas_call x1, Pallas kernels, shards(): pl.pallas_call(functools.partial(body, frames, mem_slots, left_slots, pac...  64.3 us
    pallas_call x1, Pallas kernels, shards(): pl.pallas_call(finish, out_shape=tuple((jax.ShapeDtypeStruct(*r) for r in...  1.94 us

profile of v1, /device:TPU:0, one launch (start us, length us, event | category | flops | bytes accessed | tf_op | source)
XLA Modules:
  0.0 66.9 jit_solution(14009843764278811805)
XLA Ops:
  0.6 64.3 %shard_map.156 = (bf16[160,1024]{1,0:T(8,128)(2,1)}, bf16[32,1024]{1,0:T(8,128)(2,1)}, bf16[32,4,512]{2,1,0:T(4,128)(2,1)}, bf16[32,4,512]{2,1,0:T(4,128)(2,1)}) custom-call(bf16[5,64,512]{2,1,0:T(8,128)(2,1)} %f_hbm.1, s32[32]{0:T(128)} %fill_hbm.1, s32[32]{0:T(128)} %length_hbm.1, f32[1,1024]{1,0:T(1,128)} %bitcast.6, bf16[1024,1024]{1,0:T(8,128)(2,1)} %bitcast.5, ...), custom_call_target="tpu_custom_call" | custom-call | tf_op jit(solution)/shard_map/pallas_call | solution.py:578
  64.9 1.9 %shard_map.157 = (bf16[160,1024]{1,0:T(8,128)(2,1)}, bf16[32,1024]{1,0:T(8,128)(2,1)}, bf16[32,4,512]{2,1,0:T(4,128)(2,1)}, bf16[32,4,512]{2,1,0:T(4,128)(2,1)}) custom-call(bf16[160,1024]{1,0:T(8,128)(2,1)} %get-tuple-element.12.rows_ref, bf16[32,1024]{1,0:T(8,128)(2,1)} %get-tuple-element.13.mem_ref, bf16[32,4,512]{2,1,0:T(4,128)(2,1)} %get-tuple-element.14.keys_ref, ...), custom_call_target="tpu_custom_call" | custom-call | tf_op jit(solution)/shard_map/pallas_call | solution.py:643

commit v2 on v1

v2 whole, which is shorter than its diff:
```python
import functools

import jax
import jax.numpy as jnp
from jax import lax
from jax.experimental import pallas as pl
from jax.experimental.pallas import tpu as pltpu
from jax.sharding import PartitionSpec as P

HD = 64
GROUP = 4
ROWS = 8
KEYS = 128
FIRST = 3
LEAD = 8
UNROLL = 8

epsilon = 1e-05
masked_score = -1e30
MESH = pl.DeviceIdType.MESH
bf16 = jnp.bfloat16
f32 = jnp.float32


def normalize(values):
    average = jnp.mean(values, axis=-1, keepdims=True)
    centred = values - average
    variance = jnp.mean(centred * centred, axis=-1, keepdims=True)
    return centred * lax.rsqrt(variance + epsilon)


def matmul(left, right):
    return jnp.dot(left, right, preferred_element_type=f32)


def body(
    frames,
    mem_slots,
    left_slots,
    packed,
    f_hbm,
    fill_hbm,
    length_hbm,
    gain_hbm,
    mem_hbm,
    lk_hbm,
    lv_hbm,
    wq_hbm,
    wk_hbm,
    wv_hbm,
    wo_hbm,
    wu_hbm,
    wd_hbm,
    out_hbm,
    mnext_hbm,
    ck_hbm,
    cv_hbm,
    mnext_ref,
    ck_ref,
    cv_ref,
    f_ref,
    fill_ref,
    length_ref,
    gain_ref,
    x_ref,
    outbox,
    inbox,
    far,
    own,
    mem_v,
    lk_v,
    lv_v,
    mk,
    mv,
    gk,
    gv,
    qs,
    s_buf,
    p_buf,
    rows_v,
    att,
    hid,
    hn,
    hn_far,
    act,
    act_far,
    dacc,
    dacc_far,
    part,
    peer,
    far_out,
    far_in,
    own_out,
    own_in,
    back_out,
    back_in,
    out_v,
    send_sem,
    recv_sem,
    psend_sem,
    precv_sem,
    load_sem,
    f_sem,
    hello,
    store_sem,
):
    d = lax.axis_index("dp")
    m = lax.axis_index("mp")
    f = lax.axis_index("fsdp")
    total, width = rows_v.shape
    streams = total // ROWS
    count = frames * streams
    half = count // 2
    n_blocks, depth, cols = far.shape
    n_ff = (n_blocks - 4) // 2
    n_hid = n_ff * cols
    quarter = depth // 4
    c1 = quarter // 4
    c2 = (quarter - c1) // 2
    ybit = lax.rem(d, 2)
    zbit = lax.rem(lax.div(d, 2), 2)
    p = lax.rem(d, 4)
    py = p + 1 - 2 * ybit
    pz = p + 2 - 4 * zbit
    pd = 3 - p
    xdev = (d, m, 1 - f)
    ydev = (d + 1 - 2 * ybit, m, f)
    zdev = (d + 2 - 4 * zbit, m, f)
    mdev = (d, 1 - m, f)

    part_cols = cols // 2
    ups = [4 + j for j in range(n_ff)]
    downs = [4 + n_ff + j for j in range(n_ff)]
    order = [(b, h) for b in (0, 1, 2, 3, *ups) for h in (0, 1)]
    order += [(b, h) for h in (0, 1) for b in downs]
    n_units = len(order)
    unit_of = {pair: u for u, pair in enumerate(order)}

    def own_hbm(u, start, size, side):
        b, h = order[u]
        shift = h * part_cols
        r = pl.ds(pl.multiple_of(start, 16), size)
        lanes = pl.ds(shift, part_cols)
        if b < 4:
            return (wq_hbm, wk_hbm, wv_hbm, wo_hbm)[b].at[r, lanes]
        if b in ups:
            first = side * n_hid + (b - ups[0]) * cols
            return wu_hbm.at[r, pl.ds(pl.multiple_of(first + shift, 128), part_cols)]
        first = side * n_hid + (b - downs[0]) * cols
        return wd_hbm.at[pl.ds(pl.multiple_of(start + first, 16), size), lanes]

    def own_block(b):
        if b < 4:
            return (wq_hbm, wk_hbm, wv_hbm, wo_hbm)[b]
        if b in ups:
            first = pl.multiple_of(f * n_hid + (b - ups[0]) * cols, 128)
            return wu_hbm.at[:, pl.ds(first, cols)]
        first = pl.multiple_of(f * n_hid + (b - downs[0]) * cols, 128)
        return wd_hbm.at[pl.ds(first, depth), :]

    def piece(u, start, size):
        b, h = order[u]
        lanes = pl.ds(h * part_cols, part_cols)
        return far.at[b, pl.ds(pl.multiple_of(start, 16), size), lanes]

    sends = []

    def remote(src, dst, s_sem, r_sem, dev):
        return pltpu.make_async_remote_copy(
            src_ref=src,
            dst_ref=dst,
            send_sem=s_sem,
            recv_sem=r_sem,
            device_id=dev,
            device_id_type=MESH,
        )

    def push(src, dst, i, dev):
        copy = remote(src, dst, psend_sem.at[i], precv_sem.at[i], dev)
        copy.start()
        sends.append(copy)

    def landed(ref, i):
        remote(ref, ref, psend_sem.at[i], precv_sem.at[i], xdev).wait_recv()

    def send(src, u, start, size, dev, kind):
        half_of = (2 * u) // n_units
        dst = piece(u, start, size)
        remote(src, dst, send_sem.at[half_of], recv_sem.at[u, kind], dev).start()

    def arrived(u, start, size, kind):
        ref = piece(u, start, size)
        remote(ref, ref, send_sem.at[0], recv_sem.at[u, kind], xdev).wait_recv()

    def load(src, dst, i):
        copy = pltpu.make_async_copy(src, dst, load_sem.at[i])
        copy.start()
        return copy

    n_fsdp = lax.axis_size("fsdp")
    me = d * n_fsdp + f
    wbit = lax.rem(lax.div(d, 4), 2)

    def across(mask):
        x, y, z, w = mask
        to_d = d + y * (1 - 2 * ybit) + 2 * z * (1 - 2 * zbit) + 4 * w * (1 - 2 * wbit)
        to_f = f + x * (1 - 2 * f)
        return (to_d, m, to_f), to_d * n_fsdp + to_f

    barrier = pltpu.get_barrier_semaphore()
    greeted = [xdev, ydev, zdev, mdev]
    if packed:
        greeted.append(across((0, 0, 0, 1))[0])
    for dev in greeted:
        pl.semaphore_signal(barrier, inc=1, device_id=dev, device_id_type=MESH)

    f_load = load(f_hbm, f_ref if packed else x_ref, n_blocks + 3)
    small_loads = [
        load(fill_hbm, fill_ref, n_blocks + 4),
        load(length_hbm, length_ref, n_blocks + 5),
        load(gain_hbm, gain_ref, n_blocks + 6),
    ]

    if packed:
        f_load.wait()
        pairs = outbox.shape[1]
        for k in range(pairs):
            low = f_ref[2 * k].astype(f32)
            high = f_ref[min(2 * k + 1, frames - 1)].astype(f32)
            turned = jnp.concatenate([low, high], axis=0).T.astype(bf16)
            outbox[:, k] = turned.reshape(outbox.shape[0], streams, turned.shape[1])

    with jax.named_scope("barwait"):
        pl.semaphore_wait(barrier, len(greeted))

    def send_own(u):
        if u >= n_units:
            return
        send(own_hbm(u, p * quarter, quarter, 1 - f), u, p * quarter, quarter, xdev, 0)
        send(own_hbm(u, pd * quarter, c1, 1 - f), u, pd * quarter, c1, xdev, 2)

    for u in range(FIRST):
        send_own(u)
    share = streams // 2

    def slot(box, i, side):
        return box.at[i, :, pl.ds(pl.multiple_of(side * share, 16), share), :]

    known = (
        ((1, 0, 0, 0), (0, 1, 0, 0), (0, 0, 1, 0), (0, 0, 0, 1)),
        ((1, 0, 1, 0), (0, 1, 1, 0), (0, 0, 1, 1)),
        ((1, 1, 0, 0), (0, 1, 0, 1), (0, 1, 1, 1), (1, 1, 1, 0)),
        ((1, 0, 0, 1), (1, 0, 1, 1), (1, 1, 0, 1), (1, 1, 1, 1)),
    )
    masks = [mask for group in known for mask in group]

    if packed:
        for i, group in enumerate(known):
            if i > 0:
                dev = (zdev, ydev, xdev)[i - 1]
                with jax.named_scope("hello%d" % i):
                    pl.semaphore_signal(
                        hello.at[i - 1], inc=1, device_id=dev, device_id_type=MESH
                    )
                    pl.semaphore_wait(hello.at[i - 1], 1)
            for mask in group:
                dev, index = across(mask)
                remote(
                    slot(outbox, index, m), slot(inbox, me, m), f_sem.at[0], f_sem.at[1], dev
                ).start()
    for u in range(FIRST, LEAD):
        send_own(u)

    loads = [load(own_block(b), own.at[b], b) for b in range(n_blocks)]
    mem_load = load(mem_hbm, mem_v, n_blocks)
    lk_load = load(lk_hbm, lk_v, n_blocks + 1)
    lv_load = load(lv_hbm, lv_v, n_blocks + 2)

    def pass_quarter(u):
        if u >= n_units:
            return
        arrived(u, p * quarter, quarter, 0)
        send_own(u + LEAD)
        src = piece(u, p * quarter, quarter)
        send(src, u, p * quarter, quarter, ydev, 1)
        send(src, u, p * quarter, quarter, zdev, 1)

    def pass_diagonal(u):
        if u < 0 or u >= n_units:
            return
        arrived(u, 0, 2 * quarter, 1)
        at_y = pz * quarter + c1
        send(piece(u, at_y, c2), u, at_y, c2, ydev, 2)
        at_z = py * quarter + c1 + c2
        send(piece(u, at_z, c2), u, at_z, c2, zdev, 2)

    def complete(u):
        arrived(u, pd * quarter, quarter, 2)
        if order[u][1] == 0 and order[u][0] not in downs:
            loads[order[u][0]].wait()

    pumped = [0]

    def pump(to):
        while pumped[0] <= to:
            u = pumped[0]
            with jax.named_scope("pump%d" % u):
                pass_diagonal(u - 2)
                pass_quarter(u)
            pumped[0] = u + 1

    mine = pl.ds(pl.multiple_of(f * depth, 128), depth)
    other = pl.ds(pl.multiple_of((1 - f) * depth, 128), depth)

    pump(3)

    others = inbox.at[pl.ds(0, max(inbox.shape[0] - 1, 1)), :, pl.ds(0, share), :]

    def features_in():
        inbox[pl.ds(me, 1)] = outbox[pl.ds(me, 1)]
        with jax.named_scope("fwait"):
            remote(others, others, f_sem.at[0], f_sem.at[1], xdev).wait_recv()
        for mask in masks:
            ref = slot(inbox, across(mask)[1], m)
            remote(ref, ref, f_sem.at[2], f_sem.at[3], mdev).start()

    def features_out():
        with jax.named_scope("gwait"):
            remote(others, others, f_sem.at[2], f_sem.at[3], xdev).wait_recv()
        lane_half = inbox.shape[3] // 2
        for t in range(frames):
            k, side = t // 2, t % 2
            lanes = slice(side * lane_half, side * lane_half + lane_half)
            x_ref[t * streams : (t + 1) * streams, :] = jnp.concatenate(
                [inbox[i, k][:, lanes] for i in range(inbox.shape[0])], axis=1
            )

    packed_rows = count + streams

    def normalize_rows():
        summed = None
        major = []
        for t in range(frames):
            n = normalize(x_ref[t * streams : (t + 1) * streams, :].astype(f32)).astype(bf16)
            major.append(n)
            if t < GROUP:
                summed = n.astype(f32) if t == 0 else summed + n.astype(f32)
        major.append((summed * (1.0 / GROUP)).astype(bf16))
        major = jnp.concatenate(major, axis=0)
        r_id = lax.broadcasted_iota(jnp.int32, (total, packed_rows), 0)
        c_id = lax.broadcasted_iota(jnp.int32, (total, packed_rows), 1)
        frame_id = r_id % ROWS
        target = jnp.where(frame_id <= frames, frame_id * streams + r_id // ROWS, -1)
        spread_rows = jnp.where(target == c_id, 1.0, 0.0).astype(bf16)
        rows_v[...] = matmul(spread_rows, major).astype(bf16)

    def lanes_of(h):
        return slice(h * part_cols, (h + 1) * part_cols)

    def project(b, h):
        sums = matmul(rows_v[:, mine], own[b, :, lanes_of(h)])
        sums = sums + matmul(rows_v[:, other], far[b, :, lanes_of(h)])
        return sums.astype(bf16).astype(f32)

    def project_memory(b, h, target):
        step = 512

        @pl.loop(0, mem_v.shape[0] // step)
        def _(i):
            r = pl.ds(pl.multiple_of(i * step, step), step)
            sums = matmul(mem_v[r, mine], own[b, :, lanes_of(h)])
            sums = sums + matmul(mem_v[r, other], far[b, :, lanes_of(h)])
            target[r, lanes_of(h)] = sums.astype(bf16)

    def await_unit(b, h):
        u = unit_of[b, h]
        pump(max(u + 2, min(u + 3, 5)))
        with jax.named_scope("c%d" % u):
            complete(u)

    def store(src, dst, i):
        copy = pltpu.make_async_copy(src, dst, store_sem.at[i])
        copy.start()
        return copy

    def project_group(b, h, target, kept):
        values = project(b, h).reshape(streams, ROWS, part_cols)
        kept[:, :, lanes_of(h)] = values[:, :GROUP].astype(bf16)
        padded = jnp.concatenate([values, jnp.zeros_like(values)], axis=1)
        target[:, lanes_of(h)] = padded.reshape(2 * total, part_cols).astype(bf16)

    heads = part_cols // HD
    span = heads * ROWS
    lanes3 = lax.broadcasted_iota(jnp.int32, (heads, ROWS, part_cols), 2)
    head3 = lax.broadcasted_iota(jnp.int32, (heads, ROWS, part_cols), 0)
    head_mask = jnp.where(lanes3 // HD == head3, 1.0, 0.0).astype(f32)
    row2 = lax.broadcasted_iota(jnp.int32, (span, KEYS), 0)
    lane2 = lax.broadcasted_iota(jnp.int32, (span, KEYS), 1)
    excluded = jnp.where((row2 % ROWS == frames) & (lane2 < mem_slots), -1.0, 0.0).astype(f32)
    lane1 = lax.broadcasted_iota(jnp.int32, (1, KEYS), 1)
    left_end = mem_slots + left_slots
    pad = jnp.zeros((KEYS - mem_slots - left_slots - 2 * ROWS, part_cols), bf16)
    scale = HD ** (-0.5)

    def gather_rows(mem_part, left_part, group_part, s, h):
        return jnp.concatenate(
            [
                mem_part[pl.ds(pl.multiple_of(s * mem_slots, mem_slots), mem_slots), lanes_of(h)],
                left_part[s, :, lanes_of(h)],
                group_part[pl.ds(pl.multiple_of(s * 2 * ROWS, 2 * ROWS), 2 * ROWS), lanes_of(h)],
                pad,
            ],
            axis=0,
        )

    def stream_rows(s):
        return pl.ds(pl.multiple_of(s * ROWS, ROWS), ROWS)

    def score_rows(s):
        return pl.ds(pl.multiple_of(s * span, span), span)

    def score(s, h):
        spread = (qs[stream_rows(s), lanes_of(h)][None] * head_mask).reshape(span, part_cols)
        k = gather_rows(mk, lk_v, gk, s, h)
        scores = lax.dot_general(
            spread.astype(bf16), k, (((1,), (1,)), ((), ())), preferred_element_type=f32
        )
        first_mem = mem_slots - fill_ref[s]
        first_left = left_end - length_ref[s]
        first = jnp.where(lane1 < mem_slots, first_mem, first_left)
        first = jnp.where(lane1 < left_end, first, 0)
        hide1 = (lane1 < first) | (lane1 >= left_end + frames)
        hide = jnp.where(hide1, -1.0, 0.0) + excluded
        s_buf[score_rows(s), :] = jnp.where(hide < 0.0, masked_score, scores * scale)

    def soften(h):
        step = 256

        @pl.loop(0, s_buf.shape[0] // step)
        def _(i):
            r = pl.ds(pl.multiple_of(i * step, step), step)
            scores = s_buf[r, :]
            e = jnp.exp(scores - jnp.max(scores, axis=-1, keepdims=True))
            p_buf[h, r, :] = (e / jnp.sum(e, axis=-1, keepdims=True)).astype(bf16)

    def combine(s, h):
        v = gather_rows(mv, lv_v, gv, s, h)
        o = matmul(p_buf[h, score_rows(s), :], v).reshape(heads, ROWS, part_cols) * head_mask
        att[stream_rows(s), lanes_of(h)] = jnp.sum(o, axis=0)

    def each_stream(do, h):
        @pl.loop(0, streams // UNROLL)
        def _(i):
            for t in range(UNROLL):
                do(i * UNROLL + t, h)

    if packed:
        features_in()
    else:
        f_load.wait()
    await_unit(0, 0)
    if packed:
        features_out()
    with jax.named_scope("norm"):
        normalize_rows()
    with jax.named_scope("q0"):
        qs[:, lanes_of(0)] = project(0, 0)
    await_unit(0, 1)
    with jax.named_scope("q1"):
        qs[:, lanes_of(1)] = project(0, 1)
    for copy in [mem_load, lk_load, lv_load] + small_loads:
        copy.wait()
    for h in (0, 1):
        await_unit(1, h)
        with jax.named_scope("mk%d" % h):
            project_memory(1, h, mk)
        pump(6 + 2 * h)
        with jax.named_scope("gk%d" % h):
            project_group(1, h, gk, ck_ref)
        with jax.named_scope("score%d" % h):
            each_stream(score, h)
        pump(7 + 2 * h)
        with jax.named_scope("soft%d" % h):
            soften(h)
    stores = [store(ck_ref, ck_hbm, 0)]
    for h in (0, 1):
        await_unit(2, h)
        with jax.named_scope("mv%d" % h):
            project_memory(2, h, mv)
        pump(10 + h)
        with jax.named_scope("gv%d" % h):
            project_group(2, h, gv, cv_ref)
        with jax.named_scope("comb%d" % h):
            each_stream(combine, h)
    stores.append(store(cv_ref, cv_hbm, 1))

    def both(b):
        await_unit(b, 0)
        await_unit(b, 1)

    both(3)
    with jax.named_scope("oproj"):
        r_id = lax.broadcasted_iota(jnp.int32, (packed_rows, total), 0)
        c_id = lax.broadcasted_iota(jnp.int32, (packed_rows, total), 1)
        pick = (r_id % streams) * ROWS + r_id // streams
        gather = jnp.where(pick == c_id, 1.0, 0.0).astype(bf16)
        attended = matmul(gather, att[...].astype(bf16)).astype(bf16)
        part[:, mine] = matmul(attended, own[3]).astype(bf16)
        part[:, other] = matmul(attended, far[3]).astype(bf16)
    push(part, peer, 0, mdev)
    pump(12)
    with jax.named_scope("ex0"):
        landed(peer, 0)

    my_half = pl.multiple_of(m * half, 16)
    its_half = pl.multiple_of((1 - m) * half, 16)
    rows_mine = pl.ds(my_half, half)
    rows_its = pl.ds(its_half, half)

    def residual(r):
        h = x_ref[r, :].astype(f32) + (part[r, :].astype(f32) + peer[r, :].astype(f32))
        hid[r, :] = h
        hn[r, :] = normalize(h).astype(bf16)

    with jax.named_scope("hid"):
        residual(rows_mine)
        push(hn.at[rows_mine, :], hn_far.at[rows_mine, :], 1, xdev)
        pump(13)
        residual(rows_its)
        s = slice(count, packed_rows)
        mnext_ref[...] = jnp.tanh(part[s, :].astype(f32) + peer[s, :].astype(f32)).astype(bf16)
        stores.append(store(mnext_ref, mnext_hbm, 2))

    def up(rows, target, j):
        sums = matmul(rows[:, mine], own[ups[j]]) + matmul(rows[:, other], far[ups[j]])
        target[:, j * cols : (j + 1) * cols] = jax.nn.gelu(sums, approximate=True).astype(bf16)

    def down(rows, weights, lanes):
        sums = None
        for j in range(n_ff):
            term = matmul(rows[:, j * cols : (j + 1) * cols], weights[downs[j], :, lanes])
            sums = term if sums is None else sums + term
        return sums

    pump(14)
    for j in range(n_ff):
        both(ups[j])
        with jax.named_scope("up%d" % j):
            up(hn, act, j)
        pump(15 + j)
    with jax.named_scope("hnwait"):
        landed(hn_far.at[rows_mine, :], 1)
        push(hn_far.at[rows_mine, :], hn_far.at[rows_mine, :], 2, mdev)
        landed(hn_far.at[rows_its, :], 2)
    with jax.named_scope("farup"):
        for j in range(n_ff):
            up(hn_far, act_far, j)
    pump(n_units + 1)

    shift = pl.multiple_of((1 - f) * depth, 128)
    spans = [(own, slice(0, cols), mine)]
    for h in (0, 1):
        spans.append((far, lanes_of(h), pl.ds(shift + h * part_cols, part_cols)))

    for b in downs:
        loads[b].wait()
    for i, (weights, lanes, dst) in enumerate(spans):
        if i > 0:
            for b in downs:
                await_unit(b, i - 1)
        with jax.named_scope("fardn%d" % i):
            sums = down(act_far, weights, lanes)
            dacc_far[:, dst] = sums
            far_out[rows_its, dst] = dacc_far[rows_its, dst].astype(bf16)
        push(far_out.at[rows_its, dst], far_in.at[rows_its, dst], 3 + 2 * i, mdev)
        with jax.named_scope("owndn%d" % i):
            dacc[:, dst] = down(act, weights, lanes)
            own_out[:, dst] = dacc[:, dst].astype(bf16)
        if i == len(spans) - 1:
            push(own_out, own_in, 9, mdev)
        with jax.named_scope("xsum%d" % i):
            landed(far_in.at[rows_mine, dst], 3 + 2 * i)
            both_sums = dacc_far[rows_mine, dst] + far_in[rows_mine, dst].astype(f32)
            back_out[:, dst] = both_sums.astype(bf16)
        push(back_out.at[:, dst], back_in.at[:, dst], 4 + 2 * i, xdev)
    with jax.named_scope("ownsum"):
        landed(own_in, 9)
        y = hid[rows_mine, :] + (dacc[rows_mine, :] + own_in[rows_mine, :].astype(f32))
        hid[rows_mine, :] = y
    with jax.named_scope("xwait"):
        for i, (_, _, dst) in enumerate(spans):
            landed(back_in.at[:, dst], 4 + 2 * i)
    with jax.named_scope("final"):
        y = hid[rows_mine, :] + back_in[...].astype(f32)
        out_v[rows_mine, :] = (normalize(y) * gain_ref[...]).astype(bf16)
    push(out_v.at[rows_mine, :], out_v.at[rows_mine, :], 10, mdev)
    stores.append(store(out_v.at[rows_mine, :], out_hbm.at[rows_mine, :], 3))
    with jax.named_scope("lastwait"):
        landed(out_v.at[rows_its, :], 10)
    stores.append(store(out_v.at[rows_its, :], out_hbm.at[rows_its, :], 4))

    with jax.named_scope("sendwait"):
        for copy in sends:
            copy.wait_send()
        for i in range(2):
            ref = far.at[pl.ds(i * (n_blocks // 2), n_blocks // 2), :, :]
            remote(ref, ref, send_sem.at[i], recv_sem.at[0, 0], xdev).wait_send()
        if packed:
            for i in (0, 2):
                remote(others, others, f_sem.at[i], f_sem.at[1], xdev).wait_send()
        for copy in stores:
            copy.wait()


def finish(rows_hbm, mem_hbm, keys_hbm, vals_hbm, out_hbm, mnext_hbm, ck_hbm, cv_hbm, *scratch):
    buffers, (in_sem, out_sem) = scratch[:4], scratch[4:]
    arrays = (
        (rows_hbm, buffers[0], out_hbm),
        (mem_hbm, buffers[1], mnext_hbm),
        (keys_hbm, buffers[2], ck_hbm),
        (vals_hbm, buffers[3], cv_hbm),
    )
    ins = [pltpu.make_async_copy(a, b, in_sem.at[i]) for i, (a, b, _) in enumerate(arrays)]
    outs = [pltpu.make_async_copy(b, c, out_sem.at[i]) for i, (_, b, c) in enumerate(arrays)]
    for copy in ins:
        copy.start()
    for first, second in zip(ins, outs):
        first.wait()
        second.start()
    for copy in outs:
        copy.wait()


def shards(
    features,
    memory_bank,
    memory_fill,
    left_keys,
    left_values,
    left_length,
    w_query,
    w_key,
    w_value,
    w_out,
    w_up,
    w_down,
    out_gain,
):
    frames, width_dev, all_streams = features.shape
    streams, mem_slots, width = memory_bank.shape
    left_slots = left_keys.shape[1]
    depth, cols = w_query.shape
    n_dp = lax.axis_size("dp")
    n_fsdp = lax.axis_size("fsdp")
    n_ff = w_up.shape[1] // (n_fsdp * cols)
    n_blocks = 4 + 2 * n_ff
    total = streams * ROWS
    count = frames * streams
    peers = n_dp * n_fsdp
    packed = 2 * width_dev == KEYS and streams % 32 == 0 and n_dp == 8 and n_fsdp == 2
    if packed:
        feed = features
    else:
        flat = features.reshape(frames * width_dev, all_streams)
        got = lax.all_to_all(flat, ("dp", "fsdp"), split_axis=1, concat_axis=0, tiled=True)
        got = got.reshape(peers, frames, width_dev, streams)
        feed = jnp.transpose(got, (1, 3, 0, 2)).reshape(count, width)
    slots = (peers, (frames + 1) // 2, streams, KEYS) if packed else (1, 1, 32, KEYS)
    hbm = pl.BlockSpec(memory_space=pl.ANY)
    results = (
        ((count, width), bf16),
        ((streams, width), bf16),
        ((streams, GROUP, cols), bf16),
        ((streams, GROUP, cols), bf16),
    )
    middle = pl.pallas_call(
        functools.partial(body, frames, mem_slots, left_slots, packed),
        out_shape=tuple(jax.ShapeDtypeStruct(*r) for r in results),
        in_specs=[hbm] * 13,
        out_specs=(hbm,) * 4,
        scratch_shapes=[pltpu.VMEM(*r) for r in results[1:]]
        + [
            pltpu.VMEM(features.shape if packed else (1, 16, KEYS), bf16),
            pltpu.SMEM((streams,), jnp.int32),
            pltpu.SMEM((streams,), jnp.int32),
            pltpu.VMEM((1, width), f32),
            pltpu.VMEM((count, width), bf16),
            pltpu.VMEM(slots, bf16),
            pltpu.VMEM(slots, bf16),
            pltpu.VMEM((n_blocks, depth, cols), bf16),
            pltpu.VMEM((n_blocks, depth, cols), bf16),
            pltpu.VMEM((streams * mem_slots, width), bf16),
            pltpu.VMEM(left_keys.shape, bf16),
            pltpu.VMEM(left_keys.shape, bf16),
            pltpu.VMEM((streams * mem_slots, cols), bf16),
            pltpu.VMEM((streams * mem_slots, cols), bf16),
            pltpu.VMEM((2 * total, cols), bf16),
            pltpu.VMEM((2 * total, cols), bf16),
            pltpu.VMEM((total, cols), f32),
            pltpu.VMEM((streams * ROWS * cols // (2 * HD), KEYS), f32),
            pltpu.VMEM((2, streams * ROWS * cols // (2 * HD), KEYS), bf16),
            pltpu.VMEM((total, width), bf16),
            pltpu.VMEM((total, cols), f32),
            pltpu.VMEM((count, width), f32),
            pltpu.VMEM((count, width), bf16),
            pltpu.VMEM((count, width), bf16),
            pltpu.VMEM((count, n_ff * cols), bf16),
            pltpu.VMEM((count, n_ff * cols), bf16),
            pltpu.VMEM((count, width), f32),
            pltpu.VMEM((count, width), f32),
            pltpu.VMEM((count + streams, width), bf16),
            pltpu.VMEM((count + streams, width), bf16),
            pltpu.VMEM((count, width), bf16),
            pltpu.VMEM((count, width), bf16),
            pltpu.VMEM((count, width), bf16),
            pltpu.VMEM((count, width), bf16),
            pltpu.VMEM((count // 2, width), bf16),
            pltpu.VMEM((count // 2, width), bf16),
            pltpu.VMEM((count, width), bf16),
            pltpu.SemaphoreType.DMA((2,)),
            pltpu.SemaphoreType.DMA((2 * n_blocks, 3)),
            pltpu.SemaphoreType.DMA((11,)),
            pltpu.SemaphoreType.DMA((11,)),
            pltpu.SemaphoreType.DMA((n_blocks + 7,)),
            pltpu.SemaphoreType.DMA((4,)),
            pltpu.SemaphoreType.REGULAR((3,)),
            pltpu.SemaphoreType.DMA((5,)),
        ],
        compiler_params=pltpu.CompilerParams(
            collective_id=0, has_side_effects=True, vmem_limit_bytes=60 * 1024 * 1024
        ),
    )(
        feed,
        memory_fill,
        left_length,
        out_gain.reshape(1, width),
        memory_bank.reshape(streams * mem_slots, width),
        left_keys,
        left_values,
        w_query,
        w_key,
        w_value,
        w_out,
        w_up,
        w_down,
    )
    layer_out, memory_next, center_keys, center_values = pl.pallas_call(
        finish,
        out_shape=tuple(jax.ShapeDtypeStruct(*r) for r in results),
        in_specs=[hbm] * 4,
        out_specs=(hbm,) * 4,
        scratch_shapes=[pltpu.VMEM(*r) for r in results] + [pltpu.SemaphoreType.DMA((4,))] * 2,
        compiler_params=pltpu.CompilerParams(vmem_limit_bytes=60 * 1024 * 1024),
    )(*middle)
    layer_out = jnp.transpose(layer_out.reshape(frames, streams, width), (1, 0, 2))
    return (layer_out, memory_next, center_keys, center_values)


def solution(mesh):
    in_specs = (
        P(None, ("dp", "fsdp"), None),
        P(("dp", "fsdp"), None, None),
        P(("dp", "fsdp")),
        P(("dp", "fsdp"), None, "mp"),
        P(("dp", "fsdp"), None, "mp"),
        P(("dp", "fsdp")),
        P("fsdp", "mp"),
        P("fsdp", "mp"),
        P("fsdp", "mp"),
        P("mp", "fsdp"),
        P("fsdp", "mp"),
        P("mp", "fsdp"),
        P(),
    )
    out_specs = (
        P(("dp", "fsdp"), None, None),
        P(("dp", "fsdp"), None),
        P(("dp", "fsdp"), None, "mp"),
        P(("dp", "fsdp"), None, "mp"),
    )
    return jax.shard_map(shards, mesh=mesh, in_specs=in_specs, out_specs=out_specs, check_vma=False)
```

time: 67.1 us -> 58 us (0.86)
  Pallas kernels: 66.2 us -> 56.7 us
    pallas_call x1, Pallas kernels: 64.3 us -> 54.8 us  [shards(): pl.pallas_call(functools.partial(body, frames, mem_slots, left_slots, pac...]
where the time goes in v2:
time: 58 us; the launch traced here: 57.3 us
  Pallas kernels  56.7 us (98%)
  between operations  0.64 us (1%)
    pallas_call x1, Pallas kernels, shards(): pl.pallas_call(functools.partial(body, frames, mem_slots, left_slots, pac...  54.8 us
    pallas_call x1, Pallas kernels, shards(): pl.pallas_call(finish, out_shape=tuple((jax.ShapeDtypeStruct(*r) for r in...  1.87 us

profile of v2, /device:TPU:0, one launch (start us, length us, event | category | flops | bytes accessed | tf_op | source)
XLA Modules:
  0.0 57.3 jit_solution(2374735340966199222)
XLA Ops:
  0.6 54.8 %shard_map.156 = (bf16[160,1024]{1,0:T(8,128)(2,1)}, bf16[32,1024]{1,0:T(8,128)(2,1)}, bf16[32,4,512]{2,1,0:T(4,128)(2,1)}, bf16[32,4,512]{2,1,0:T(4,128)(2,1)}) custom-call(bf16[5,64,512]{2,1,0:T(8,128)(2,1)} %f_hbm.1, s32[32]{0:T(128)} %fill_hbm.1, s32[32]{0:T(128)} %length_hbm.1, f32[1,1024]{1,0:T(1,128)} %bitcast.6, bf16[1024,1024]{1,0:T(8,128)(2,1)} %bitcast.5, ...), custom_call_target="tpu_custom_call" | custom-call | tf_op jit(solution)/shard_map/pallas_call | solution.py:676
  55.4 1.9 %shard_map.157 = (bf16[160,1024]{1,0:T(8,128)(2,1)}, bf16[32,1024]{1,0:T(8,128)(2,1)}, bf16[32,4,512]{2,1,0:T(4,128)(2,1)}, bf16[32,4,512]{2,1,0:T(4,128)(2,1)}) custom-call(bf16[160,1024]{1,0:T(8,128)(2,1)} %get-tuple-element.12.rows_hbm, bf16[32,1024]{1,0:T(8,128)(2,1)} %get-tuple-element.13.mem_hbm, bf16[32,4,512]{2,1,0:T(4,128)(2,1)} %get-tuple-element.14.keys_hbm, ...), custom_call_target="tpu_custom_call" | custom-call | tf_op jit(solution)/shard_map/pallas_call | solution.py:747
